TPU v7x, 256 devices: a whole 4x4x8 slice. The times are simulated.
256 devices in a mesh: img: 16 (over x, z_lo, core), tp: 16 (over y, z_hi).
Axes of the slice: x: 4, y: 4, z: 8 (z_hi: 4, z_lo: 2; z = z_hi * 2 + z_lo), core: 2. Of those that a mesh axis runs over, the one named last changes fastest.
Arguments:
- patch_tokens: bfloat16 [32768, 1024], P(('img', 'tp')), may hold values from -12 to 12
- norm_gain: float32 [1024], replicated, may hold values from 0.1 to 1.9
- norm_bias: float32 [1024], replicated, may hold values from -3 to 3
- up_weight: bfloat16 [1024, 8192], P('img', 'tp'), may hold values from -0.1875 to 0.1875
- up_bias: float32 [8192], P('tp'), may hold values from -3 to 3
- down_weight: bfloat16 [8192, 4096], P('tp', 'img'), may hold values from -0.125 to 0.125
- down_bias: float32 [4096], replicated, may hold values from -3 to 3
Outputs:
- projected: bfloat16 [32768, 4096], P(('img', 'tp'))
All inputs are finite; a program needn't handle non-finite values.
Results may differ from a plain program's by a relative error of at most 0.014.
Values may be sent and summed in bfloat16 or wider, within the bound.
No kernel may reach another device: no remote copies, remote signals or barrier semaphores. Data moves between devices by JAX's collectives and lax.ppermute only.
A program may use at most 128 MiB of HBM per device.

v0:
```python
import jax
import jax.numpy as jnp
from jax import lax
from jax.sharding import PartitionSpec as P


def laid_out(parts, dim):
    dims = list(parts.shape[1:])
    dims[dim] *= parts.shape[0]
    return jnp.moveaxis(parts, 0, dim).reshape(dims)


def from_everyone(x, axis):
    copies = jnp.broadcast_to(x, (lax.axis_size(axis), *x.shape))
    return lax.all_to_all(copies, axis, split_axis=0, concat_axis=0, tiled=True)


def gather_directly(x, axis, dim):
    return laid_out(from_everyone(x, axis), dim)


def on_device(patch_tokens, norm_gain, norm_bias, up_weight, up_bias, down_weight, down_bias):
    values = lax.all_gather(patch_tokens, "tp", axis=0, tiled=True).astype(jnp.float32)
    center = jnp.mean(values, axis=1, keepdims=True)
    spread = jnp.mean((values - center) ** 2, axis=1, keepdims=True)
    gathered = ((values - center) * lax.rsqrt(spread + 1e-05) * norm_gain + norm_bias).astype(
        jnp.bfloat16
    )
    summed = jnp.dot(
        gathered, gather_directly(up_weight, "img", 0), preferred_element_type=jnp.float32
    )
    hidden = jax.nn.gelu(summed + up_bias).astype(jnp.bfloat16)
    down_full = lax.all_gather(down_weight, "img", axis=1, tiled=True)
    total = lax.psum_scatter(
        jnp.dot(hidden, down_full, preferred_element_type=jnp.float32).astype(jnp.bfloat16),
        "tp",
        scatter_dimension=0,
        tiled=True,
    ).astype(jnp.float32)
    return (total + down_bias).astype(jnp.bfloat16)


def solution(mesh):
    return jax.shard_map(
        on_device,
        mesh=mesh,
        in_specs=(P(("img", "tp"), None), P(), P(), P("img", "tp"), P("tp"), P("tp", "img"), P()),
        out_specs=P(("img", "tp"), None),
        check_vma=False,
    )
```

profile of v0, /device:TPU:1, one launch (start us, length us, event | category | flops | bytes accessed | tf_op | source)
XLA Modules:
  0.0 372.6 jit_solution(12355794440621910350)
XLA Ops:
  6.5 0.0 all-gather.3.cloned.1.call-start
  6.5 0.7 all-gather.3.cloned.1.call-update
  7.3 0.0 all-gather.5.cloned.1.call-start
  7.3 0.7 all-gather.5.cloned.1.call-update
  8.0 1.9 broadcast_in_dim.2
  9.9 7.2 %all-to-all-start = ((bf16[16,64,512]{2,1,0:T(8,128)(2,1)}), bf16[16,64,512]{2,1,0:T(8,128)(2,1)S(1)}, u32[]{:S(2)}, u32[]{:S(2)}) async-start(bf16[16,64,512]{2,1,0:T(8,128)(2,1)} %broadcast_in_dim.2), calls=%async_computation | async-start | bytes 2097152 | tf_op jit(solution)/shard_map/all_to_all | solution.py:15
  17.1 0.0 copy-start.2
  17.1 0.0 copy-start.3
  17.1 0.0 copy-start.4
  17.1 0.0 reduce-scatter.2.cloned.1.call-start
  17.2 72.1 %all-gather.3.cloned.1.call-done = bf16[2048,1024]{1,0:T(8,128)(2,1)} async-done(((bf16[128,1024]{1,0:T(8,128)(2,1)}), bf16[2048,1024]{1,0:T(8,128)(2,1)}) %all-gather.3.cloned.1.call-update) | async-done | bytes 4194320 | tf_op jit(solution)/shard_map/all_gather | solution.py:23
  89.2 0.0 copy-start
  89.2 3.0 convert_reduce_fusion
  92.2 0.5 copy-done
  92.7 1.4 fusion.2
  94.1 0.0 all-to-all-done
  94.1 47.1 %all-gather.5.cloned.1.call-done = bf16[512,4096]{1,0:T(8,128)(2,1)} async-done(((bf16[512,256]{1,0:T(8,128)(2,1)}), bf16[512,4096]{1,0:T(8,128)(2,1)}) %all-gather.5.cloned.1.call-update) | async-done | bytes 4194320 | tf_op jit(solution)/shard_map/all_gather | solution.py:33
  141.1 0.0 copy-done.2
  141.1 0.0 copy-done.3
  141.1 0.0 copy-done.4
  141.1 18.0 %convolution_convert_fusion = bf16[2048,4096]{1,0:T(8,128)(2,1)} fusion(bf16[512,4096]{1,0:T(8,128)(2,1)} %all-gather.5.cloned.1.call-done, bf16[1024,512]{1,0:T(8,128)(2,1)S(1)} %bitcast.3, bf16[2048,1024]{1,0:T(8,128)(2,1)} %all-gather.3.cloned.1.call-done, f32[1024]{0:T(1024)S(1)} %copy-done.2, f32[1024]{0:T(1024)S(1)} %copy-done.3, ...), kind=kOutput, calls=%fused_computation | convolution fusion | flops 10768875520 | bytes 26241024 | tf_op jit(solution)/shard_map/dot_general | solution.py:35
  159.1 0.0 copy-start.1
  159.1 0.0 reduce-scatter.2.cloned.1.call-update
  159.1 204.5 %reduce-scatter.2.cloned.1.call-done = bf16[128,4096]{1,0:T(8,128)(2,1)} async-done(((bf16[2048,4096]{1,0:T(8,128)(2,1)}), bf16[128,4096]{1,0:T(8,128)(2,1)}) %reduce-scatter.2.cloned.1.call-update) | async-done | bytes 1048592 | tf_op jit(solution)/shard_map/reduce_scatter | solution.py:34
  363.7 0.0 copy-done.1
  363.7 2.4 add_convert_fusion
  (2 shorter events, 0.0 us)
Async XLA Ops:
  6.5 82.7 %all-gather.3.cloned.1.call-start = ((), (), s32[]{:S(2)}) async-start(), calls=%async_computation.2 | async-start | bytes 4456448 | tf_op jit(solution)/shard_map/all_gather | solution.py:23
  7.3 133.9 %all-gather.5.cloned.1.call-start = ((), (), s32[]{:S(2)}) async-start(), calls=%async_computation.3 | async-start | bytes 4456448 | tf_op jit(solution)/shard_map/all_gather | solution.py:33
  9.9 84.1 %all-to-all-start = ((bf16[16,64,512]{2,1,0:T(8,128)(2,1)}), bf16[16,64,512]{2,1,0:T(8,128)(2,1)S(1)}, u32[]{:S(2)}, u32[]{:S(2)}) async-start(bf16[16,64,512]{2,1,0:T(8,128)(2,1)} %broadcast_in_dim.2), calls=%async_computation | async-start | bytes 2097152 | tf_op jit(solution)/shard_map/all_to_all | solution.py:15
  17.1 124.0 %copy-start.2 = (f32[1024]{0:T(1024)S(1)}, f32[1024]{0:T(1024)}, u32[]{:S(2)}) copy-start(f32[1024]{0:T(1024)} %param.9) | copy-start | bytes 12292
  17.1 124.0 %copy-start.3 = (f32[1024]{0:T(1024)S(1)}, f32[1024]{0:T(1024)}, u32[]{:S(2)}) copy-start(f32[1024]{0:T(1024)} %param.8) | copy-start | bytes 12292
  17.1 124.0 %copy-start.4 = (f32[512]{0:T(512)S(1)}, f32[512]{0:T(512)}, u32[]{:S(2)}) copy-start(f32[512]{0:T(512)} %param.11) | copy-start | bytes 6148
  17.1 346.6 %reduce-scatter.2.cloned.1.call-start = ((), (), s32[]{:S(2)}) async-start(), calls=%async_computation.4 | async-start | bytes 17825792 | tf_op jit(solution)/shard_map/reduce_scatter | solution.py:34
  89.2 3.4 copy-start
  159.1 204.6 %copy-start.1 = (f32[4096]{0:T(1024)S(1)}, f32[4096]{0:T(1024)}, u32[]{:S(2)}) copy-start(f32[4096]{0:T(1024)} %param.13) | copy-start | bytes 49156
Sparse Core Ops, SparseCore 0:
  9.8 79.4 all-gather.2
  91.0 50.1 all-gather.4
  159.3 204.3 reduce-scatter.1
where the time goes:
time: 373 us
  waiting for transfers between devices  325 us (87%)
  matrix products  18 us (5%)
  between operations  13.2 us (4%)
  starting transfers between devices  7.24 us (2%)
  other arithmetic  6.74 us (2%)
    reduce_scatter x1, waiting for transfers between devices, on_device(): lax.psum_scatter(jnp.dot(hidden, down_full, preferred_element_type=jnp.fl...  205 us
    all_gather x1, waiting for transfers between devices, on_device(): lax.all_gather(patch_tokens, 'tp', axis=0, tiled=True).astype(jnp.float32)  72.1 us
    all_gather x1, waiting for transfers between devices, on_device(): down_full = lax.all_gather(down_weight, 'img', axis=1, tiled=True)  47.1 us
    dot_general x1, matrix products, on_device(): jnp.dot(hidden, down_full, preferred_element_type=jnp.float32)  18 us
  transfers between devices with their start and end apart: 4, of which 3 were waited for; matrix products, arithmetic and copies ran while one was open for 2% of the time, Pallas kernels for 0%

commit v1 on v0

--- a/solution.py
+++ b/solution.py
@@ -30,7 +30,10 @@
         gathered, gather_directly(up_weight, "img", 0), preferred_element_type=jnp.float32
     )
     hidden = jax.nn.gelu(summed + up_bias).astype(jnp.bfloat16)
-    down_full = lax.all_gather(down_weight, "img", axis=1, tiled=True)
+    n_dev = lax.axis_size("img")
+    blocks = jnp.stack([down_weight for _ in range(n_dev)])
+    blocks = lax.all_to_all(blocks, "img", split_axis=0, concat_axis=0)
+    down_full = jnp.concatenate(blocks, axis=1)
     total = lax.psum_scatter(
         jnp.dot(hidden, down_full, preferred_element_type=jnp.float32).astype(jnp.bfloat16),
         "tp",

time: 373 us -> 359 us (0.962)
  waiting for transfers between devices: 325 us -> 302 us
  starting transfers between devices: 7.24 us -> 12.5 us
    all_gather x1 -> x0, waiting for transfers between devices: 47.1 us -> none  [on_device(): down_full = lax.all_gather(down_weight, 'img', axis=1, tiled=True)]
    all_to_all x1, waiting for transfers between devices: 0.01 us -> 13.8 us  [from_everyone(): return lax.all_to_all(copies, axis, split_axis=0, concat_axis=0, tiled=True)]
    all_to_all x0 -> x1, waiting for transfers between devices: none -> 6.47 us  [on_device(): blocks = lax.all_to_all(blocks, 'img', split_axis=0, concat_axis=0)]
    all_to_all x0 -> x1, starting transfers between devices: none -> 5.25 us  [on_device(): blocks = lax.all_to_all(blocks, 'img', split_axis=0, concat_axis=0)]
    all_gather x1, waiting for transfers between devices: 72.1 us -> 77.1 us  [on_device(): lax.all_gather(patch_tokens, 'tp', axis=0, tiled=True).astype(jnp.float32)]
  transfers between devices with their start and end apart: 4 -> 4, of which waited for: 3 -> 4; matrix products, arithmetic and copies ran while one was open for 2% -> 2% of each run, Pallas kernels for 0% -> 0%
where the time goes in v1:
time: 359 us; the launch traced here: 358 us
  waiting for transfers between devices  302 us (84%)
  matrix products  17.9 us (5%)
  between operations  13.5 us (4%)
  starting transfers between devices  12.5 us (3%)
  other arithmetic  6.74 us (2%)
  local copies, waits for them, and re-layouts  5.85 us (2%)
    reduce_scatter x1, waiting for transfers between devices, on_device(): lax.psum_scatter(jnp.dot(hidden, down_full, preferred_element_type=jnp.fl...  204 us
    all_gather x1, waiting for transfers between devices, on_device(): lax.all_gather(patch_tokens, 'tp', axis=0, tiled=True).astype(jnp.float32)  77.1 us
    dot_general x1, matrix products, on_device(): jnp.dot(hidden, down_full, preferred_element_type=jnp.float32)  17.9 us
    all_to_all x1, waiting for transfers between devices, from_everyone(): return lax.all_to_all(copies, axis, split_axis=0, concat_axis=0, tiled=True)  13.8 us
  transfers between devices with their start and end apart: 4, of which 4 were waited for; matrix products, arithmetic and copies ran while one was open for 2% of the time, Pallas kernels for 0%

profile of v1, /device:TPU:1, one launch (start us, length us, event | category | flops | bytes accessed | tf_op | source)
XLA Modules:
  0.0 358.5 jit_solution(2266810811509428176)
XLA Ops:
  6.5 1.9 broadcast_in_dim.2
  8.4 7.2 %all-to-all-start = ((bf16[16,64,512]{2,1,0:T(8,128)(2,1)}), bf16[16,64,512]{2,1,0:T(8,128)(2,1)S(1)}, u32[]{:S(2)}, u32[]{:S(2)}) async-start(bf16[16,64,512]{2,1,0:T(8,128)(2,1)} %broadcast_in_dim.2), calls=%async_computation | async-start | bytes 2097152 | tf_op jit(solution)/shard_map/all_to_all | solution.py:15
  15.6 0.0 all-gather.2.cloned.1.call-start
  15.6 0.7 all-gather.2.cloned.1.call-update
  16.3 1.1 copy.8
  17.4 13.8 %all-to-all-done = bf16[16,64,512]{2,1,0:T(8,128)(2,1)S(1)} async-done(((bf16[16,64,512]{2,1,0:T(8,128)(2,1)}), bf16[16,64,512]{2,1,0:T(8,128)(2,1)S(1)}, u32[]{:S(2)}, u32[]{:S(2)}) %all-to-all-start) | async-done | bytes 1048608 | tf_op jit(solution)/shard_map/all_to_all | solution.py:15
  31.3 2.4 stack.2
  33.6 5.2 %all-to-all-start.1 = ((bf16[16,512,256]{1,2,0:T(8,128)(2,1)}), bf16[16,512,256]{1,2,0:T(8,128)(2,1)}, u32[]{:S(2)}, u32[]{:S(2)}) async-start(bf16[16,512,256]{1,2,0:T(8,128)(2,1)} %stack.2), calls=%async_computation.1 | async-start | bytes 8388608 | tf_op jit(solution)/shard_map/all_to_all | solution.py:35
  38.9 0.0 copy-start.2
  38.9 0.0 copy-start.3
  38.9 0.0 copy-start.4
  38.9 0.0 reduce-scatter.2.cloned.1.call-start
  38.9 77.1 %all-gather.2.cloned.1.call-done = bf16[2048,1024]{1,0:T(8,128)(2,1)} async-done(((bf16[128,1024]{1,0:T(8,128)(2,1)}), bf16[2048,1024]{1,0:T(8,128)(2,1)}) %all-gather.2.cloned.1.call-update) | async-done | bytes 4194320 | tf_op jit(solution)/shard_map/all_gather | solution.py:23
  116.1 0.0 copy-start
  116.1 3.0 convert_reduce_fusion
  119.0 0.5 copy-done
  119.5 1.4 fusion.2
  120.9 6.5 %all-to-all-done.1 = bf16[16,512,256]{1,2,0:T(8,128)(2,1)} async-done(((bf16[16,512,256]{1,2,0:T(8,128)(2,1)}), bf16[16,512,256]{1,2,0:T(8,128)(2,1)}, u32[]{:S(2)}, u32[]{:S(2)}) %all-to-all-start.1) | async-done | bytes 4194336 | tf_op jit(solution)/shard_map/all_to_all | solution.py:35
  127.4 0.0 copy-done.2
  127.4 0.0 copy-done.3
  127.4 0.0 copy-done.4
  127.4 17.9 %convolution_convert_fusion = bf16[2048,4096]{1,0:T(8,128)(2,1)} fusion(bf16[512,4096]{0,1:T(8,128)(2,1)} %bitcast.2, bf16[1024,512]{1,0:T(8,128)(2,1)S(1)} %bitcast.6, bf16[2048,1024]{1,0:T(8,128)(2,1)} %all-gather.2.cloned.1.call-done, f32[1024]{0:T(1024)S(1)} %copy-done.2, f32[1024]{0:T(1024)S(1)} %copy-done.3, f32[2048]{0:T(1024)S(1)} %add_rsqrt_fusion, ...), kind=kOutput, calls=%fused_computation | convolution fusion | flops 10768875520 | bytes 26241024 | tf_op jit(solution)/shard_map/dot_general | solution.py:38
  145.3 0.0 copy-start.1
  145.3 0.0 reduce-scatter.2.cloned.1.call-update
  145.4 203.9 %reduce-scatter.2.cloned.1.call-done = bf16[128,4096]{1,0:T(8,128)(2,1)} async-done(((bf16[2048,4096]{1,0:T(8,128)(2,1)}), bf16[128,4096]{1,0:T(8,128)(2,1)}) %reduce-scatter.2.cloned.1.call-update) | async-done | bytes 1048592 | tf_op jit(solution)/shard_map/reduce_scatter | solution.py:37
  349.3 0.0 copy-done.1
  349.3 2.4 add_convert_fusion
  (2 shorter events, 0.0 us)
Async XLA Ops:
  8.4 22.8 %all-to-all-start = ((bf16[16,64,512]{2,1,0:T(8,128)(2,1)}), bf16[16,64,512]{2,1,0:T(8,128)(2,1)S(1)}, u32[]{:S(2)}, u32[]{:S(2)}) async-start(bf16[16,64,512]{2,1,0:T(8,128)(2,1)} %broadcast_in_dim.2), calls=%async_computation | async-start | bytes 2097152 | tf_op jit(solution)/shard_map/all_to_all | solution.py:15
  15.6 100.5 %all-gather.2.cloned.1.call-start = ((), (), s32[]{:S(2)}) async-start(), calls=%async_computation.3 | async-start | bytes 4456448 | tf_op jit(solution)/shard_map/all_gather | solution.py:23
  33.6 93.8 %all-to-all-start.1 = ((bf16[16,512,256]{1,2,0:T(8,128)(2,1)}), bf16[16,512,256]{1,2,0:T(8,128)(2,1)}, u32[]{:S(2)}, u32[]{:S(2)}) async-start(bf16[16,512,256]{1,2,0:T(8,128)(2,1)} %stack.2), calls=%async_computation.1 | async-start | bytes 8388608 | tf_op jit(solution)/shard_map/all_to_all | solution.py:35
  38.9 88.5 %copy-start.2 = (f32[1024]{0:T(1024)S(1)}, f32[1024]{0:T(1024)}, u32[]{:S(2)}) copy-start(f32[1024]{0:T(1024)} %param.9) | copy-start | bytes 12292
  38.9 88.5 %copy-start.3 = (f32[1024]{0:T(1024)S(1)}, f32[1024]{0:T(1024)}, u32[]{:S(2)}) copy-start(f32[1024]{0:T(1024)} %param.8) | copy-start | bytes 12292
  38.9 88.5 %copy-start.4 = (f32[512]{0:T(512)S(1)}, f32[512]{0:T(512)}, u32[]{:S(2)}) copy-start(f32[512]{0:T(512)} %param.11) | copy-start | bytes 6148
  38.9 310.4 %reduce-scatter.2.cloned.1.call-start = ((), (), s32[]{:S(2)}) async-start(), calls=%async_computation.4 | async-start | bytes 17825792 | tf_op jit(solution)/shard_map/reduce_scatter | solution.py:37
  116.1 3.4 copy-start
  145.3 203.9 %copy-start.1 = (f32[4096]{0:T(1024)S(1)}, f32[4096]{0:T(1024)}, u32[]{:S(2)}) copy-start(f32[4096]{0:T(1024)} %param.13) | copy-start | bytes 49156
Sparse Core Ops, SparseCore 0:
  18.8 97.1 all-gather.1
  145.5 203.7 reduce-scatter.1
